TPU v7x, 32 devices: a whole 2x2x4 slice. The times are simulated.
32 devices in a mesh: fsdp: 4 (over y, x), tp: 2 (over core), rep: 4 (over z).
Axes of the slice: x: 2, y: 2, z: 4, core: 2. Of those that a mesh axis runs over, the one named last changes fastest.
Arguments:
- tokens: bfloat16 [4096, 5120], P('fsdp', 'rep'), may hold values from -6 to 6
- ref_qkv: bfloat16 [5120, 7168], P(('rep', 'fsdp'), 'tp'), may hold values from -0.078125 to 0.078125
- ref_bias: float32 [7168], P('tp'), may hold values from -9 to 9
- segment_ids: int32 [4, 1024], P('fsdp'), may hold values from 0 to 7, never falling along the last dimension, each value on 1 to 512 neighbouring positions
- policy_key: bfloat16 [5120, 1024], P(('rep', 'fsdp'), 'tp'), may hold values from -0.078125 to 0.078125
Outputs:
- context: bfloat16 [4096, 5120], P(('fsdp', 'rep'), 'tp')
- policy_key_tp: bfloat16 [5120, 1024], P(None, 'tp')
All inputs are finite; a program needn't handle non-finite values.
Results may differ from a plain program's by a relative error of at most 0.0093.
Values may be sent and summed in bfloat16 or wider, within the bound.
A program may use at most 128 MiB of HBM per device.

v0:
```python
import jax
import jax.numpy as jnp
from jax import lax
from jax.sharding import PartitionSpec as P

QH = 40
KVH = 8
HD = 128


def positions_of(seg):
    count = seg.shape[0]
    index = jnp.arange(count, dtype=jnp.int32)
    starts = jnp.concatenate([jnp.ones((1,), bool), seg[1:] != seg[:-1]])
    first = lax.cummax(jnp.where(starts, index, 0), axis=0)
    return index - first


def rotary(values, pos):
    half = values.shape[-1] // 2
    freq = 1000000.0 ** (-2.0 * jnp.arange(half, dtype=jnp.float32) / values.shape[-1])
    angle = pos.astype(jnp.float32)[:, None] * freq[None, :]
    shape = (values.shape[0],) + (1,) * (values.ndim - 2) + (half,)
    cosine = jnp.cos(angle).reshape(shape)
    sine = jnp.sin(angle).reshape(shape)
    first = values[..., :half]
    second = values[..., half:]
    return jnp.concatenate(
        [first * cosine - second * sine, second * cosine + first * sine], axis=-1
    )


def per_device(tokens, ref_qkv, ref_bias, segment_ids, policy_key):
    share = QH // KVH
    rows = tokens.shape[0]
    columns = ref_qkv.shape[1]
    groups = columns // ((share + 2) * HD)
    replicas = lax.axis_size("rep")
    mine = rows // replicas
    rank = lax.axis_index("rep")
    partial_value = jnp.dot(
        tokens,
        lax.all_gather(ref_qkv, "fsdp", axis=0, tiled=True),
        preferred_element_type=jnp.float32,
    )
    partial_value = partial_value.reshape(rows, groups, share + 2, HD)
    bias = ref_bias.reshape(groups, share + 2, HD)
    seg = segment_ids[0]
    pos = positions_of(seg)
    start = rank * mine
    my_pos = lax.dynamic_slice_in_dim(pos, start, mine, 0)
    summed = lax.psum_scatter(partial_value, "rep", scatter_dimension=0, tiled=True) + bias[None]
    query = rotary(summed[:, :, :share], my_pos).astype(jnp.bfloat16)
    my_keys = rotary(summed[:, :, share], my_pos).astype(jnp.bfloat16)
    my_vals = summed[:, :, share + 1].astype(jnp.bfloat16)
    keys, vals = (
        lax.all_gather(my_keys, "rep", axis=0, tiled=True),
        lax.all_gather(my_vals, "rep", axis=0, tiled=True),
    )
    scores = jnp.einsum(
        "qhgd,khd->hgqk", query, keys, preferred_element_type=jnp.float32
    ) / jnp.sqrt(jnp.float32(HD))
    query_index = start + jnp.arange(mine, dtype=jnp.int32)
    key_index = jnp.arange(rows, dtype=jnp.int32)
    my_seg = lax.dynamic_slice_in_dim(seg, start, mine, 0)
    allowed = (my_seg[:, None] == seg[None, :]) & (key_index[None, :] <= query_index[:, None])
    scores = jnp.where(allowed[None, None], scores, -1e30)
    top = jnp.max(scores, axis=-1, keepdims=True)
    expo = jnp.exp(scores - top)
    weights = (expo / jnp.sum(expo, axis=-1, keepdims=True)).astype(jnp.bfloat16)
    context = jnp.einsum("hgqk,khd->qhgd", weights, vals, preferred_element_type=jnp.float32)
    context = context.astype(jnp.bfloat16).reshape(mine, groups * share * HD)
    inner = lax.all_gather(policy_key, "rep", axis=0, tiled=True)
    outer = lax.all_gather(inner, "fsdp", axis=0, tiled=True)
    blocks = policy_key.shape[0]
    shards = outer.shape[0] // (blocks * replicas)
    whole = (
        outer.reshape(shards, replicas, blocks, outer.shape[1])
        .transpose(1, 0, 2, 3)
        .reshape(outer.shape)
    )
    return (context, whole)


def solution(mesh):
    in_specs = (
        P("fsdp", "rep"),
        P(("rep", "fsdp"), "tp"),
        P("tp"),
        P("fsdp", None),
        P(("rep", "fsdp"), "tp"),
    )
    out_specs = (P(("fsdp", "rep"), "tp"), P(None, "tp"))
    return jax.shard_map(
        per_device, mesh=mesh, in_specs=in_specs, out_specs=out_specs, check_vma=False
    )
```

profile of v0, /device:TPU:0, one launch (start us, length us, event | category | flops | bytes accessed | tf_op | source)
XLA Modules:
  0.0 530.3 jit_solution(14261949471272091948)
XLA Ops:
  7.2 0.0 copy-start
  7.2 0.0 all-gather.7.cloned.1.call-start
  7.2 0.7 all-gather.7.cloned.1.call-update
  7.9 0.0 all-gather.11.cloned.1.call-start
  8.0 0.7 all-gather.11.cloned.1.call-update
  8.7 0.0 reduce-scatter.2.cloned.1.call-start
  8.7 97.9 %all-gather.7.cloned.1.call-done = bf16[1280,3584]{1,0:T(8,128)(2,1)} async-done(((bf16[320,3584]{1,0:T(8,128)(2,1)}), bf16[1280,3584]{1,0:T(8,128)(2,1)}) %all-gather.7.cloned.1.call-update) | async-done | bytes 9175056 | tf_op jit(solution)/shard_map/all_gather | solution.py:43
  106.6 0.0 copy-done
  106.6 15.2 %fusion.29 = f32[1024,3584]{0,1:T(8,128)} fusion(bf16[1024,1280]{1,0:T(8,128)(2,1)S(1)} %copy-done, bf16[1280,3584]{1,0:T(8,128)(2,1)} %all-gather.7.cloned.1.call-done), kind=kOutput, calls=%fused_computation.42 | convolution fusion | flops 9395240960 | bytes 26476544 | tf_op jit(solution)/shard_map/dot_general | solution.py:41
  121.8 15.2 %copy.13 = f32[1024,4,7,128]{3,0,2,1:T(8,128)} copy(f32[1024,4,7,128]{0,3,2,1:T(8,128)} %bitcast.53) | data formatting | bytes 29360128 | tf_op jit(solution)/shard_map/reshape | solution.py:46
  137.0 0.0 copy-start.4
  137.0 0.0 copy-start.3
  137.0 0.0 reduce-scatter.2.cloned.1.call-update
  137.0 0.0 all-gather.13.cloned.1.call-start
  137.1 3.6 all-gather.11.cloned.1.call-done
  140.7 0.0 all-gather.13.cloned.1.call-update
  140.7 0.0 all-gather.9.cloned.1.call-start
  140.8 0.0 copy-done.4
  140.8 0.0 copy-done.3
  140.8 0.1 compare_reduce_fusion
  140.9 0.1 add_select_fusion
  141.0 0.3 reduce-window.9
  141.3 0.1 slice.42
  141.4 0.1 slice_reduce_fusion
  141.5 0.1 bitcast_subtract_fusion
  141.6 0.1 dynamic-slice_convert_fusion
  141.7 0.5 multiply_cosine_fusion
  142.2 245.7 %reduce-scatter.2.cloned.1.call-done = f32[256,4,7,128]{3,0,2,1:T(8,128)} async-done(((f32[1024,4,7,128]{3,0,2,1:T(8,128)}), f32[256,4,7,128]{3,0,2,1:T(8,128)}) %reduce-scatter.2.cloned.1.call-update) | async-done | bytes 3670032 | tf_op jit(solution)/shard_map/reduce_scatter | solution.py:52
  387.9 2.5 broadcast_add_fusion
  390.4 0.0 copy-start.2
  390.4 1.8 copy-done.2
  392.2 0.3 subtract_convert_fusion.1
  392.5 0.9 pad_maximum_fusion.1
  393.4 0.0 all-gather.9.cloned.1.call-update
  393.4 0.2 all-gather.15.cloned.1.call-start
  393.6 0.3 fusion.17
  393.9 58.1 %all-gather.13.cloned.1.call-done = bf16[5120,512]{1,0:T(8,128)(2,1)} async-done(((bf16[1280,512]{1,0:T(8,128)(2,1)}), bf16[5120,512]{1,0:T(8,128)(2,1)}) %all-gather.13.cloned.1.call-update) | async-done | bytes 5242896 | tf_op jit(solution)/shard_map/all_gather | solution.py:74
  452.0 5.3 %copy.16 = bf16[4,4,320,512]{3,2,0,1:T(8,128)(2,1)} copy(bf16[4,4,320,512]{3,2,1,0:T(8,128)(2,1)} %bitcast.54) | data formatting | bytes 10485760 | tf_op jit(solution)/shard_map/reshape | solution.py:78
  457.3 1.8 slice.67
  459.1 0.0 all-gather.15.cloned.1.call-update
  459.1 3.7 subtract_convert_fusion
  462.8 19.2 %all-gather.9.cloned.1.call-done = bf16[1024,4,128]{2,0,1:T(8,128)(2,1)} async-done(((bf16[256,4,128]{2,0,1:T(8,128)(2,1)}), bf16[1024,4,128]{2,0,1:T(8,128)(2,1)}) %all-gather.9.cloned.1.call-update) | async-done | bytes 1048592 | tf_op jit(solution)/shard_map/all_gather | solution.py:57
  482.0 12.1 %fusion.24 = (f32[4,5,256]{2,1,0:T(8,128)S(1)}, f32[4,5,256,1024]{2,3,1,0:T(8,128)}) fusion(pred[256,1024]{0,1:T(8,128)(4,1)S(1)} %fusion.17, bf16[1024,4,128]{2,0,1:T(8,128)(2,1)} %all-gather.9.cloned.1.call-done, bf16[256,4,5,64]{3,0,2,1:T(8,128)(2,1)S(1)} %get-tuple-element.7, bf16[256,4,5,64]{3,0,2,1:T(8,128)(2,1)S(1)} %get-tuple-element.6), kind=kOutput, calls=%fused_computation.41 | convolution fusion | flops 1365771264 | bytes 23613440 | tf_op jit(solution)/shard_map/sub | solution.py:69
  494.2 16.7 %all-gather.15.cloned.1.call-done = bf16[1024,4,1,128]{3,0,2,1:T(8,128)(2,1)} async-done(((bf16[256,4,1,128]{3,0,2,1:T(8,128)(2,1)}), bf16[1024,4,1,128]{3,0,2,1:T(8,128)(2,1)}) %all-gather.15.cloned.1.call-update) | async-done | bytes 1048592 | tf_op jit(solution)/shard_map/all_gather | solution.py:58
  510.8 0.0 copy-start.1
  510.8 10.2 %fusion.8 = bf16[4,128,5,256]{3,1,2,0:T(8,128)(2,1)} fusion(f32[4,5,256,1024]{2,3,1,0:T(8,128)} %get-tuple-element.13, f32[4,5,256]{2,1,0:T(8,128)S(1)} %get-tuple-element.12, bf16[1024,4,1,128]{3,0,2,1:T(8,128)(2,1)} %all-gather.15.cloned.1.call-done), kind=kOutput, calls=%fused_computation.13 | convolution fusion | flops 1353318400 | bytes 23351296 | tf_op jit(solution)/shard_map/hgqk,khd->qhgd/dot_general | solution.py:71
  521.0 2.4 copy.17
  523.5 0.0 copy-done.1
  (6 shorter events, 0.1 us)
Async XLA Ops:
  7.2 99.4 %copy-start = (bf16[1024,1280]{1,0:T(8,128)(2,1)S(1)}, bf16[1024,1280]{1,0:T(8,128)(2,1)}, u32[]{:S(2)}) copy-start(bf16[1024,1280]{1,0:T(8,128)(2,1)} %param.5) | copy-start | bytes 7864324
  7.2 99.4 %all-gather.7.cloned.1.call-start = ((), (), s32[]{:S(2)}) async-start(), calls=%async_computation.1 | async-start | bytes 11468800 | tf_op jit(solution)/shard_map/all_gather | solution.py:43
  7.9 132.8 %all-gather.11.cloned.1.call-start = ((), (), s32[]{:S(2)}) async-start(), calls=%async_computation.4 | async-start | bytes 1638400 | tf_op jit(solution)/shard_map/all_gather | solution.py:73
  8.7 379.3 %reduce-scatter.2.cloned.1.call-start = ((), (), s32[]{:S(2)}) async-start(), calls=%async_computation.2 | async-start | bytes 18350080 | tf_op jit(solution)/shard_map/reduce_scatter | solution.py:52
  137.0 3.8 copy-start.4
  137.0 3.8 copy-start.3
  137.0 315.0 %all-gather.13.cloned.1.call-start = ((), (), s32[]{:S(2)}) async-start(), calls=%async_computation.5 | async-start | bytes 6553600 | tf_op jit(solution)/shard_map/all_gather | solution.py:74
  140.7 341.3 %all-gather.9.cloned.1.call-start = ((), (), s32[]{:S(2)}) async-start(), calls=%async_computation.3 | async-start | bytes 1310720 | tf_op jit(solution)/shard_map/all_gather | solution.py:57
  390.4 1.8 copy-start.2
  393.4 117.5 %all-gather.15.cloned.1.call-start = ((), (), s32[]{:S(2)}) async-start(), calls=%async_computation.6 | async-start | bytes 1310720 | tf_op jit(solution)/shard_map/all_gather | solution.py:58
  510.8 12.6 %copy-start.1 = (bf16[1024,1280]{1,0:T(8,128)(2,1)S(1)}, bf16[1024,1280]{1,0:T(8,128)(2,1)}, u32[]{:S(2)}) copy-start(bf16[1024,1280]{1,0:T(8,128)(2,1)} %param.5) | copy-start | bytes 7864324
Sparse Core Ops, SparseCore 0:
  9.8 96.7 all-gather.6
  108.2 32.5 all-gather.10
  143.1 244.8 reduce-scatter.1
  389.6 62.3 all-gather.12
  454.0 27.9 all-gather.8
  483.4 27.3 all-gather.14
where the time goes:
time: 531 us; the launch traced here: 530 us
  waiting for transfers between devices  443 us (83%)
  matrix products  37.5 us (7%)
  local copies, waits for them, and re-layouts  26.8 us (5%)
  between operations  14.2 us (3%)
  other arithmetic  8.65 us (2%)
    reduce_scatter x1, waiting for transfers between devices, per_device(): lax.psum_scatter(partial_value, 'rep', scatter_dimension=0, tiled=True)  246 us
    all_gather x1, waiting for transfers between devices, per_device(): lax.all_gather(ref_qkv, 'fsdp', axis=0, tiled=True)  97.9 us
    all_gather x1, waiting for transfers between devices, per_device(): outer = lax.all_gather(inner, 'fsdp', axis=0, tiled=True)  58.1 us
    all_gather x1, waiting for transfers between devices, per_device(): lax.all_gather(my_keys, 'rep', axis=0, tiled=True)  19.2 us
    all_gather x1, waiting for transfers between devices, per_device(): lax.all_gather(my_vals, 'rep', axis=0, tiled=True)  16.7 us
    reshape x1, local copies, waits for them, and re-layouts, per_device(): partial_value = partial_value.reshape(rows, groups, share + 2, HD)  15.2 us
    dot_general x1, matrix products, per_device(): jnp.dot(tokens, lax.all_gather(ref_qkv, 'fsdp', axis=0, tiled=True), pref...  15.2 us
    sub x1, matrix products, per_device(): expo = jnp.exp(scores - top)  12.1 us
  transfers between devices with their start and end apart: 6, of which 6 were waited for; matrix products, arithmetic and copies ran while one was open for 11% of the time, Pallas kernels for 0%

commit v1 on v0

--- a/solution.py
+++ b/solution.py
@@ -1,7 +1,13 @@
 import jax
 import jax.numpy as jnp
 from jax import lax
+from jax.experimental import pallas as pl
+from jax.experimental.pallas import tpu as pltpu
 from jax.sharding import PartitionSpec as P
+import functools
+import math
+
+MESH = pl.DeviceIdType.MESH
 
 QH = 40
 KVH = 8
@@ -82,6 +88,286 @@
     return (context, whole)
 
 
+def neighbours():
+    f, r, t = lax.axis_index("fsdp"), lax.axis_index("rep"), lax.axis_index("tp")
+    ahead = [{"rep": lax.rem(r + k, 4)} for k in range(4)]
+    fx = f - lax.rem(f, 2) + 1 - lax.rem(f, 2)
+    fy = lax.rem(f + 2, 4)
+    return f, r, t, ahead, fx, fy
+
+
+def greet(devices):
+    barrier = pltpu.get_barrier_semaphore()
+    for device in devices:
+        pl.semaphore_signal(barrier, inc=1, device_id=device, device_id_type=MESH)
+    pl.semaphore_wait(barrier, len(devices))
+
+
+class Copies:
+    def __init__(self, send, recv):
+        self.send, self.recv, self.made = send, recv, []
+
+    def start(self, src, dst, device):
+        n = len(self.made)
+        copy = pltpu.make_async_remote_copy(
+            src_ref=src, dst_ref=dst, send_sem=self.send.at[n], recv_sem=self.recv.at[n],
+            device_id=device, device_id_type=MESH,
+        )
+        copy.start()
+        self.made.append(copy)
+        return copy
+
+    def finish(self):
+        for copy in self.made:
+            copy.wait_send()
+
+
+N_GATHER = 27
+
+
+def gather_kernel(tok, w, x, wg, send, recv, local):
+    f, r, t, ahead, fx, fy = neighbours()
+    to_x, to_y, partner = {"fsdp": fx}, {"fsdp": fy}, {"tp": 1 - t}
+    greet([ahead[1], ahead[2], ahead[3], to_x, to_y, partner])
+    copies = Copies(send, recv)
+    rows, depth = tok.shape
+    block, width = wg.shape[2:]
+    half, quarter, hb = rows // 2, rows // 4, block // 2
+    source = [lax.rem(r + 4 - k, 4) for k in range(4)]
+
+    def cols(rank):
+        return pl.ds(pl.multiple_of(rank * width, 128), width)
+
+    def feats(rank):
+        return pl.ds(pl.multiple_of(rank * depth, 128), depth)
+
+    def mine(first, count):
+        return pl.ds(pl.multiple_of(t * half + first, quarter), count)
+
+    def across(src, k):
+        dst = wg.at[source[k], f]
+        return copies.start(src, dst, to_x), copies.start(src, dst, to_y)
+
+    def onward(k):
+        first, second = pl.ds(0, hb), pl.ds(hb, hb)
+        bx, by = passed[k]
+        bx.wait_recv()
+        a = copies.start(wg.at[source[k], fx, first], wg.at[source[k], fx, first], to_y)
+        by.wait_recv()
+        b = copies.start(wg.at[source[k], fy, second], wg.at[source[k], fy, second], to_x)
+        return a, b
+
+    passed = {0: across(w.at[:, cols(r)], 0)}
+    spread = {
+        k: copies.start(w.at[:, cols(lax.rem(r + k, 4))], wg.at[r, f], ahead[k])
+        for k in (1, 3, 2)
+    }
+    part = mine(0, half)
+    right = copies.start(tok.at[part], x.at[part, feats(r)], ahead[1])
+    left = copies.start(tok.at[part], x.at[part, feats(r)], ahead[3])
+    own_x = pltpu.make_async_copy(tok, x.at[:, feats(r)], local.at[0])
+    own_w = pltpu.make_async_copy(w.at[:, cols(r)], wg.at[r, f], local.at[1])
+    own_x.start()
+    own_w.start()
+    rest = []
+    for k in (1, 3):
+        spread[k].wait_recv()
+        passed[k] = across(wg.at[source[k], f], k)
+    rest += onward(0)
+    spread[2].wait_recv()
+    passed[2] = across(wg.at[source[2], f], 2)
+    rest += onward(1)
+    from_left, from_right = feats(source[1]), feats(source[3])
+    first, second = mine(0, quarter), mine(quarter, quarter)
+    right.wait_recv()
+    ring_a = copies.start(x.at[first, from_left], x.at[first, from_left], ahead[1])
+    rest.append(copies.start(x.at[part, from_left], x.at[part, from_left], partner))
+    left.wait_recv()
+    ring_b = copies.start(x.at[second, from_right], x.at[second, from_right], ahead[3])
+    rest.append(copies.start(x.at[part, from_right], x.at[part, from_right], partner))
+    rest += onward(3)
+    rest += onward(2)
+    far = feats(source[2])
+    ring_a.wait_recv()
+    rest.append(copies.start(x.at[first, far], x.at[first, far], partner))
+    ring_b.wait_recv()
+    rest.append(copies.start(x.at[second, far], x.at[second, far], partner))
+    for copy in rest:
+        copy.wait_recv()
+    own_x.wait()
+    own_w.wait()
+    copies.finish()
+
+
+def gather(tokens, ref_qkv):
+    rows, depth = tokens.shape
+    block, columns = ref_qkv.shape
+    width = columns // 4
+    any_space = pl.BlockSpec(memory_space=pl.ANY)
+    x, wg = pl.pallas_call(
+        gather_kernel,
+        out_shape=(
+            jax.ShapeDtypeStruct((rows, depth * 4), tokens.dtype),
+            jax.ShapeDtypeStruct((4, 4, block, width), ref_qkv.dtype),
+        ),
+        in_specs=[pl.BlockSpec(memory_space=pltpu.VMEM)] * 2,
+        out_specs=(any_space, any_space),
+        scratch_shapes=[
+            pltpu.SemaphoreType.DMA((N_GATHER,)),
+            pltpu.SemaphoreType.DMA((N_GATHER,)),
+            pltpu.SemaphoreType.DMA((2,)),
+        ],
+        compiler_params=pltpu.CompilerParams(collective_id=0, has_side_effects=True),
+        cost_estimate=pl.CostEstimate(flops=0, bytes_accessed=300_000_000, transcendentals=0),
+    )(tokens, ref_qkv)
+    return x, wg.reshape(16 * block, width)
+
+
+N_ATTEND = 18
+
+
+def attend_kernel(proj, bias, cosine, sine, seg_col, seg_row, pol, out, pg, keys, vals, ctx, send, recv, local):
+    f, r, t, ahead, fx, fy = neighbours()
+    to_x, to_y = {"fsdp": fx}, {"fsdp": fy}
+    greet([ahead[1], ahead[2], ahead[3], to_x, to_y])
+    copies = Copies(send, recv)
+    rows = proj.shape[0]
+    mine = rows // 4
+    share = proj.shape[1] // HD - 2
+    block, width = pol.shape
+    hb, hw = block // 2, width // 2
+    lo, hi = pl.ds(0, hw), pl.ds(hw, hw)
+    top, low = pl.ds(0, hb), pl.ds(hb, hb)
+    behind, front, far = lax.rem(r + 3, 4), lax.rem(r + 1, 4), lax.rem(r + 2, 4)
+
+    own_p = pltpu.make_async_copy(pol, pg.at[r, f], local.at[0])
+    own_p.start()
+    b_x = copies.start(pol.at[:, hi], pg.at[r, f, :, hi], to_x)
+    b_y = copies.start(pol.at[:, hi], pg.at[r, f, :, hi], to_y)
+    a_z = [copies.start(pol.at[:, lo], pg.at[r, f, :, lo], ahead[k]) for k in (1, 3, 2)]
+
+    def rotated(values, at):
+        return values * cosine[at, :] + pltpu.roll(values, HD // 2, 1) * sine[at, :]
+
+    def column(j):
+        return pl.ds(pl.multiple_of(j * HD, HD), HD)
+
+    for i in range(4):
+        at = pl.ds(i * mine, mine)
+        kc, vc = column(share), column(share + 1)
+        keys[at, :] = rotated(proj[at, kc] + bias[:, kc], at).astype(jnp.bfloat16)
+        vals[at, :] = (proj[at, vc] + bias[:, vc]).astype(jnp.bfloat16)
+
+    span = 3 * mine
+    scale = 1.0 / math.sqrt(HD)
+
+    def attend(k):
+        d = lax.rem(r + k, 4)
+        q0 = pl.multiple_of(d * mine, mine)
+        k0 = pl.multiple_of((d // 3) * mine, mine)
+        at, window = pl.ds(q0, mine), pl.ds(k0, span)
+        q_index = q0 + lax.broadcasted_iota(jnp.int32, (mine, span), 0)
+        k_index = k0 + lax.broadcasted_iota(jnp.int32, (mine, span), 1)
+        allowed = (seg_col[at, :] == seg_row[:, window]) & (k_index <= q_index)
+        shut = jnp.where(allowed, 0.0, -1e30)
+        kk, vv = keys[window, :], vals[window, :]
+
+        def head(j, _):
+            c = column(j)
+            query = rotated(proj[at, c] + bias[:, c], at).astype(jnp.bfloat16)
+            scores = lax.dot_general(
+                query, kk, (((1,), (1,)), ((), ())), preferred_element_type=jnp.float32
+            ) * scale + shut
+            expo = jnp.exp(scores - jnp.max(scores, axis=-1, keepdims=True))
+            total = jnp.sum(expo, axis=-1, keepdims=True)
+            weights = (expo * (1.0 / total)).astype(jnp.bfloat16)
+            ctx[k, :, c] = jnp.dot(weights, vv, preferred_element_type=jnp.float32).astype(jnp.bfloat16)
+            return 0
+
+        lax.fori_loop(0, share, head, 0)
+
+    place = pl.ds(pl.multiple_of(r * share * HD, HD), share * HD)
+    rest = []
+    attend(2)
+    rest.append(copies.start(ctx.at[2], out.at[:, place], ahead[2]))
+    own_p.wait()
+    for copy in a_z:
+        copy.wait_recv()
+    a_x = copies.start(pg.at[:, f, :, lo], pg.at[:, f, :, lo], to_x)
+    a_y = copies.start(pg.at[:, f, :, lo], pg.at[:, f, :, lo], to_y)
+    b_x.wait_recv()
+    b_y.wait_recv()
+    d_x = copies.start(pg.at[r, fx, top, hi], pg.at[r, fx, top, hi], to_y)
+    d_y = copies.start(pg.at[r, fy, low, hi], pg.at[r, fy, low, hi], to_x)
+    attend(1)
+    rest.append(copies.start(ctx.at[1], out.at[:, place], ahead[1]))
+    attend(3)
+    rest.append(copies.start(ctx.at[3], out.at[:, place], ahead[3]))
+    d_x.wait_recv()
+    d_y.wait_recv()
+    z_a = copies.start(pg.at[r, :, :, hi], pg.at[r, :, :, hi], ahead[1])
+    z_b = copies.start(pg.at[r, :, :, hi], pg.at[r, :, :, hi], ahead[3])
+    attend(0)
+    own_c = pltpu.make_async_copy(ctx.at[0], out.at[:, place], local.at[1])
+    own_c.start()
+    a_x.wait_recv()
+    rest.append(copies.start(pg.at[:, fx, top, lo], pg.at[:, fx, top, lo], to_y))
+    a_y.wait_recv()
+    rest.append(copies.start(pg.at[:, fy, low, lo], pg.at[:, fy, low, lo], to_x))
+    z_a.wait_recv()
+    rest.append(copies.start(pg.at[behind, pl.ds(0, 2), :, hi], pg.at[behind, pl.ds(0, 2), :, hi], ahead[1]))
+    z_b.wait_recv()
+    rest.append(copies.start(pg.at[front, pl.ds(2, 2), :, hi], pg.at[front, pl.ds(2, 2), :, hi], ahead[3]))
+    for copy in rest:
+        copy.wait_recv()
+    own_c.wait()
+    copies.finish()
+
+
+def attend_all(proj, bias, cosine, sine, seg, policy_key):
+    rows, columns = proj.shape
+    mine, share = rows // 4, columns // HD - 2
+    block, width = policy_key.shape
+    any_space = pl.BlockSpec(memory_space=pl.ANY)
+    out, pg = pl.pallas_call(
+        attend_kernel,
+        out_shape=(
+            jax.ShapeDtypeStruct((mine, 4 * share * HD), jnp.bfloat16),
+            jax.ShapeDtypeStruct((4, 4, block, width), policy_key.dtype),
+        ),
+        in_specs=[pl.BlockSpec(memory_space=pltpu.VMEM)] * 7,
+        out_specs=(any_space, any_space),
+        scratch_shapes=[
+            pltpu.VMEM((rows, HD), jnp.bfloat16),
+            pltpu.VMEM((rows, HD), jnp.bfloat16),
+            pltpu.VMEM((4, mine, share * HD), jnp.bfloat16),
+            pltpu.SemaphoreType.DMA((N_ATTEND,)),
+            pltpu.SemaphoreType.DMA((N_ATTEND,)),
+            pltpu.SemaphoreType.DMA((2,)),
+        ],
+        compiler_params=pltpu.CompilerParams(collective_id=1, has_side_effects=True),
+        cost_estimate=pl.CostEstimate(flops=0, bytes_accessed=150_000_000, transcendentals=0),
+    )(proj, bias, cosine, sine, seg[:, None], seg[None, :], policy_key)
+    return out, pg.reshape(16 * block, width)
+
+
+def per_group(tokens, ref_qkv, ref_bias, segment_ids, policy_key):
+    rank = lax.axis_index("rep")
+    width = ref_qkv.shape[1] // 4
+    bias = lax.dynamic_slice_in_dim(ref_bias, rank * width, width, 0)[None, :]
+    seg = segment_ids[0]
+    pos = positions_of(seg)
+    half = HD // 2
+    freq = 1000000.0 ** (-2.0 * jnp.arange(half, dtype=jnp.float32) / HD)
+    angle = pos.astype(jnp.float32)[:, None] * freq[None, :]
+    cosine, sine = jnp.cos(angle), jnp.sin(angle)
+    cosine = jnp.concatenate([cosine, cosine], axis=-1)
+    sine = jnp.concatenate([-sine, sine], axis=-1)
+    x, wg = gather(tokens, ref_qkv)
+    proj = jnp.dot(x, wg, preferred_element_type=jnp.float32)
+    return attend_all(proj, bias, cosine, sine, seg, policy_key)
+
+
 def solution(mesh):
     in_specs = (
         P("fsdp", "rep"),
@@ -91,6 +377,10 @@
         P(("rep", "fsdp"), "tp"),
     )
     out_specs = (P(("fsdp", "rep"), "tp"), P(None, "tp"))
+    shape = mesh.shape
+    grouped = (
+        shape["rep"] == 4 and shape["fsdp"] == 4 and shape["tp"] == 2 and KVH == shape["tp"] * shape["rep"]
+    )
     return jax.shard_map(
-        per_device, mesh=mesh, in_specs=in_specs, out_specs=out_specs, check_vma=False
-    )
+        per_group if grouped else per_device, mesh=mesh, in_specs=in_specs, out_specs=out_specs, check_vma=False
+    )

time: 531 us -> 269 us (0.51)
  waiting for transfers between devices: 443 us -> 0 us
  Pallas kernels: 0 us -> 238 us
  matrix products: 37.5 us -> 16.8 us
  local copies, waits for them, and re-layouts: 26.8 us -> 10.2 us
  between operations: 14.2 us -> 0.67 us
    reduce_scatter x1 -> x0, waiting for transfers between devices: 246 us -> none  [per_device(): lax.psum_scatter(partial_value, 'rep', scatter_dimension=0, tiled=True)]
    pallas_call x0 -> x2, Pallas kernels: none -> 238 us  [the longest x1 145 us: gather(): pl.pallas_call(gather_kernel, out_shape=(jax.ShapeDtypeStruct((rows, dept...]
    all_gather x5 -> x0, waiting for transfers between devices: 196 us -> none  [the longest x1 97.9 us: per_device(): lax.all_gather(ref_qkv, 'fsdp', axis=0, tiled=True)]
    reshape x2 -> x0, local copies, waits for them, and re-layouts: 20.5 us -> none  [the longest x1 15.2 us: per_device(): partial_value = partial_value.reshape(rows, groups, share + 2, HD)]
    sub x1 -> x0, matrix products: 12.1 us -> none  [per_device(): expo = jnp.exp(scores - top)]
    dot_general x2 -> x1, matrix products: 25.4 us -> 16.8 us  [per_group(): proj = jnp.dot(x, wg, preferred_element_type=jnp.float32)]
  transfers between devices with their start and end apart: 6 -> 0, of which waited for: 6 -> 0; matrix products, arithmetic and copies ran while one was open for 11% -> 0% of each run, Pallas kernels for 0% -> 0%
where the time goes in v1:
time: 269 us
  Pallas kernels  238 us (88%)
  matrix products  16.8 us (6%)
  local copies, waits for them, and re-layouts  10.2 us (4%)
  other arithmetic  3.79 us (1%)
    pallas_call x1, Pallas kernels, gather(): pl.pallas_call(gather_kernel, out_shape=(jax.ShapeDtypeStruct((rows, dept...  145 us
    pallas_call x1, Pallas kernels, attend_all(): pl.pallas_call(attend_kernel, out_shape=(jax.ShapeDtypeStruct((mine, 4 *...  92.2 us
    dot_general x1, matrix products, per_group(): proj = jnp.dot(x, wg, preferred_element_type=jnp.float32)  16.8 us
    unnamed x4, local copies, waits for them, and re-layouts  7.64 us

profile of v1, /device:TPU:0, one launch (start us, length us, event | category | flops | bytes accessed | tf_op | source)
XLA Modules:
  0.0 269.2 jit_solution(6615589968873265881)
XLA Ops:
  0.6 145.4 %shard_map.68 = (bf16[1024,5120]{1,0:T(8,128)(2,1)}, bf16[4,4,320,896]{3,2,1,0:T(8,128)(2,1)}) custom-call(bf16[1024,1280]{1,0:T(8,128)(2,1)} %tok.1, bf16[320,3584]{1,0:T(8,128)(2,1)} %w.1), custom_call_target="tpu_custom_call" | custom-call | bytes 300000000 | tf_op jit(solution)/shard_map/pallas_call | solution.py:207
  146.1 0.0 copy-start
  146.1 16.8 %fusion.2.proj = f32[1024,896]{1,0:T(8,128)} fusion(bf16[1024,5120]{1,0:T(8,128)(2,1)} %get-tuple-element.6, bf16[5120,896]{1,0:T(8,128)(2,1)} %bitcast.15), kind=kOutput, calls=%fused_computation.12 | convolution fusion | flops 9395240960 | bytes 23330816 | tf_op jit(solution)/shard_map/dot_general | solution.py:367
  162.9 0.8 dynamic_slice.3
  163.7 0.6 broadcast_in_dim.9.bias
  164.3 0.0 copy-done
  164.3 0.1 compare_reduce_fusion
  164.4 0.1 add_select_fusion
  164.5 0.3 reduce-window.9
  164.8 0.1 slice.17
  164.9 0.1 slice_reduce_fusion
  165.0 0.1 fusion.1
  165.1 1.9 fusion
  167.0 1.3 pad_maximum_fusion
  168.3 1.0 copy.7.seg_col
  169.3 92.2 %shard_map.69 = (bf16[256,2560]{1,0:T(8,128)(2,1)}, bf16[4,4,320,512]{3,2,1,0:T(8,128)(2,1)}) custom-call(f32[1024,896]{1,0:T(8,128)} %fusion.2.proj, f32[1,896]{1,0:T(1,128)} %broadcast_in_dim.9.bias, f32[1024,128]{1,0:T(8,128)} %get-tuple-element.13.cosine, f32[1024,128]{1,0:T(8,128)} %get-tuple-element.14.sine, s32[1024,1]{1,0:T(8,128)} %copy.7.seg_col, ...), custom_call_target="tpu_custom_call" | custom-call | bytes 150000000 | tf_op jit(solution)/shard_map/pallas_call | solution.py:332
  261.5 2.5 copy.10
  264.0 5.2 %copy.11 = bf16[5120,512]{1,0:T(8,128)(2,1)} copy(bf16[5120,512]{1,0:T(8,128)(2,1)} %bitcast.13) | data formatting | bytes 10485760
  (2 shorter events, 0.0 us)
Async XLA Ops:
  146.1 18.2 %copy-start = (s32[1,1024]{1,0:T(1,128)S(1)}, s32[1,1024]{1,0:T(1,128)}, u32[]{:S(2)}) copy-start(s32[1,1024]{1,0:T(1,128)} %seg_row.1) | copy-start | bytes 12292

commit v2 on v0

--- a/solution.py
+++ b/solution.py
@@ -1,7 +1,13 @@
 import jax
 import jax.numpy as jnp
 from jax import lax
+from jax.experimental import pallas as pl
+from jax.experimental.pallas import tpu as pltpu
 from jax.sharding import PartitionSpec as P
+import functools
+import math
+
+MESH = pl.DeviceIdType.MESH
 
 QH = 40
 KVH = 8
@@ -82,6 +88,286 @@
     return (context, whole)
 
 
+def neighbours():
+    f, r, t = lax.axis_index("fsdp"), lax.axis_index("rep"), lax.axis_index("tp")
+    ahead = [{"rep": lax.rem(r + k, 4)} for k in range(4)]
+    fx = f - lax.rem(f, 2) + 1 - lax.rem(f, 2)
+    fy = lax.rem(f + 2, 4)
+    return f, r, t, ahead, fx, fy
+
+
+def greet(devices):
+    barrier = pltpu.get_barrier_semaphore()
+    for device in devices:
+        pl.semaphore_signal(barrier, inc=1, device_id=device, device_id_type=MESH)
+    pl.semaphore_wait(barrier, len(devices))
+
+
+class Copies:
+    def __init__(self, send, recv):
+        self.send, self.recv, self.made = send, recv, []
+
+    def start(self, src, dst, device, sends=None):
+        n = len(self.made)
+        copy = pltpu.make_async_remote_copy(
+            src_ref=src, dst_ref=dst, send_sem=self.send.at[n], recv_sem=self.recv.at[n],
+            device_id=device, device_id_type=MESH,
+        )
+        only(sends, copy.start)
+        self.made.append((copy, sends))
+        return copy
+
+    def finish(self):
+        for copy, sends in self.made:
+            only(sends, copy.wait_send)
+
+
+def only(condition, act):
+    if condition is None:
+        act()
+    else:
+        pl.when(condition)(act)
+
+
+N_COPIES = 48
+
+
+def layer_kernel(
+    tok, w, bias, cosine, sine, seg_col, seg_row, pol, out, pg,
+    x, wg, proj, keys, vals, ctx, send, recv, local,
+):
+    f, r, t, ahead, fx, fy = neighbours()
+    to_x, to_y, partner = {"fsdp": fx}, {"fsdp": fy}, {"tp": 1 - t}
+    greet([ahead[1], ahead[2], ahead[3], to_x, to_y, partner])
+    copies = Copies(send, recv)
+    rows, depth = tok.shape
+    mine, half = rows // 4, rows // 2
+    block, width = w.shape[0], wg.shape[2]
+    hb = block // 2
+    share = width // HD - 2
+    pw = pol.shape[1] // 2
+    lo, hi = pl.ds(0, pw), pl.ds(pw, pw)
+    top, low = pl.ds(0, hb), pl.ds(hb, hb)
+    source = [lax.rem(r + 4 - k, 4) for k in range(4)]
+
+    def cols(rank):
+        return pl.ds(pl.multiple_of(rank * width, 128), width)
+
+    def held(k, owner, first, count):
+        return wg.at[source[k], pl.ds(pl.multiple_of(owner * block + first, 16), count)]
+
+    def across(src, k):
+        dst = held(k, f, 0, block)
+        return copies.start(src, dst, to_x), copies.start(src, dst, to_y)
+
+    def onward(k):
+        bx, by = passed[k]
+        bx.wait_recv()
+        a = copies.start(held(k, fx, 0, hb), held(k, fx, 0, hb), to_y)
+        by.wait_recv()
+        b = copies.start(held(k, fy, hb, hb), held(k, fy, hb, hb), to_x)
+        return [a, b]
+
+    def policy_z(c):
+        return [copies.start(pol.at[:, c], pg.at[r, f, :, c], ahead[k]) for k in (1, 3, 2)]
+
+    def policy_xy(c, arrived):
+        for copy in arrived:
+            copy.wait_recv()
+        src = pg.at[:, f, :, c]
+        return copies.start(src, src, to_x), copies.start(src, src, to_y)
+
+    def policy_last(c, pair):
+        a, b = pg.at[:, fx, top, c], pg.at[:, fy, low, c]
+        pair[0].wait_recv()
+        one = copies.start(a, a, to_y)
+        pair[1].wait_recv()
+        return [one, copies.start(b, b, to_x)]
+
+    part = pl.ds(pl.multiple_of(t * half, half), half)
+
+    def line(k):
+        below, above = source[k - 1], lax.rem(r + k - 1, 4)
+        up_src = tok.at[part] if k == 1 else x.at[below, part]
+        down_src = tok.at[part] if k == 1 else x.at[above, part]
+        up = copies.start(up_src, x.at[below, part], ahead[1], (r <= 2) & (r >= k - 1))
+        down = copies.start(down_src, x.at[above, part], ahead[3], (r >= 1) & (r <= 4 - k))
+        return up, down
+
+    def landed(k, pair):
+        only(r >= k, pair[0].wait_recv)
+        only(r <= 3 - k, pair[1].wait_recv)
+
+    def to_partner(k):
+        below, above = x.at[source[k], part], x.at[lax.rem(r + k, 4), part]
+        return (
+            copies.start(below, below, partner, r >= k),
+            copies.start(above, above, partner, r <= 3 - k),
+        )
+
+    def add(left, plane):
+        def tile(i, _):
+            at = pl.ds(pl.multiple_of(i * mine, mine), mine)
+            proj[at, :] += jnp.dot(left[at, :], wg[plane], preferred_element_type=jnp.float32)
+            return 0
+
+        lax.fori_loop(0, 4, tile, 0)
+
+    def add_planes(k, pair):
+        def below():
+            pair[0].wait_recv()
+            add(x.at[source[k]], source[k])
+
+        def above():
+            pair[1].wait_recv()
+            add(x.at[lax.rem(r + k, 4)], lax.rem(r + k, 4))
+
+        only(r >= k, below)
+        only(r <= 3 - k, above)
+
+    own_w = pltpu.make_async_copy(w.at[:, cols(r)], held(0, f, 0, block), local.at[0])
+    own_p = pltpu.make_async_copy(pol, pg.at[r, f], local.at[1])
+    passed = {0: across(w.at[:, cols(r)], 0)}
+    spread = {
+        k: copies.start(w.at[:, cols(lax.rem(r + k, 4))], wg.at[r, pl.ds(pl.multiple_of(f * block, 16), block)], ahead[k])
+        for k in (1, 3, 2)
+    }
+    lo_z = policy_z(lo)
+    line1 = line(1)
+    own_w.start()
+    own_p.start()
+    proj[...] = jnp.broadcast_to(bias[...], proj.shape)
+    for k in (1, 3):
+        spread[k].wait_recv()
+        passed[k] = across(held(k, f, 0, block), k)
+    weights_in = onward(0)
+    spread[2].wait_recv()
+    passed[2] = across(held(2, f, 0, block), 2)
+    weights_in += onward(1)
+    own_p.wait()
+    lo_xy = policy_xy(lo, lo_z)
+    weights_in += onward(3)
+    landed(1, line1)
+    line2 = line(2)
+    near = to_partner(1)
+    weights_in += onward(2)
+    own_w.wait()
+    for copy in weights_in[:2]:
+        copy.wait_recv()
+    add(tok, r)
+    for copy in weights_in[2:]:
+        copy.wait_recv()
+    landed(2, line2)
+    line3 = line(3)
+    mid = to_partner(2)
+    hi_z = policy_z(hi)
+    add_planes(1, near)
+    rest = policy_last(lo, lo_xy)
+    add_planes(2, mid)
+    landed(3, line3)
+    add_planes(3, to_partner(3))
+    hi_xy = policy_xy(hi, hi_z)
+
+    def rotated(values, at):
+        return values * cosine[at, :] + pltpu.roll(values, HD // 2, 1) * sine[at, :]
+
+    def column(j):
+        return pl.ds(pl.multiple_of(j * HD, HD), HD)
+
+    for i in range(4):
+        at = pl.ds(i * mine, mine)
+        keys[at, :] = rotated(proj[at, column(share)], at).astype(jnp.bfloat16)
+        vals[at, :] = proj[at, column(share + 1)].astype(jnp.bfloat16)
+
+    span = 3 * mine
+    scale = 1.0 / math.sqrt(HD)
+
+    def attend(k):
+        d = lax.rem(r + k, 4)
+        q0 = pl.multiple_of(d * mine, mine)
+        k0 = pl.multiple_of((d // 3) * mine, mine)
+        at, window = pl.ds(q0, mine), pl.ds(k0, span)
+        q_index = q0 + lax.broadcasted_iota(jnp.int32, (mine, span), 0)
+        k_index = k0 + lax.broadcasted_iota(jnp.int32, (mine, span), 1)
+        allowed = (seg_col[at, :] == seg_row[:, window]) & (k_index <= q_index)
+        shut = jnp.where(allowed, 0.0, -1e30)
+        kk, vv = keys[window, :], vals[window, :]
+
+        def head(j, _):
+            c = column(j)
+            query = rotated(proj[at, c], at).astype(jnp.bfloat16)
+            scores = lax.dot_general(
+                query, kk, (((1,), (1,)), ((), ())), preferred_element_type=jnp.float32
+            ) * scale + shut
+            expo = jnp.exp(scores - jnp.max(scores, axis=-1, keepdims=True))
+            total = jnp.sum(expo, axis=-1, keepdims=True)
+            weights = (expo * (1.0 / total)).astype(jnp.bfloat16)
+            ctx[k, :, c] = jnp.dot(weights, vv, preferred_element_type=jnp.float32).astype(jnp.bfloat16)
+            return 0
+
+        lax.fori_loop(0, share, head, 0)
+
+    place = pl.ds(pl.multiple_of(r * share * HD, HD), share * HD)
+    for k in (2, 1, 3):
+        attend(k)
+        rest.append(copies.start(ctx.at[k], out.at[:, place], ahead[k]))
+    attend(0)
+    own_c = pltpu.make_async_copy(ctx.at[0], out.at[:, place], local.at[2])
+    own_c.start()
+    rest += policy_last(hi, hi_xy)
+    for copy in rest:
+        copy.wait_recv()
+    own_c.wait()
+    copies.finish()
+
+
+def whole_layer(tokens, ref_qkv, bias, cosine, sine, seg, policy_key):
+    rows, depth = tokens.shape
+    block, columns = ref_qkv.shape
+    width = columns // 4
+    mine, share = rows // 4, width // HD - 2
+    any_space = pl.BlockSpec(memory_space=pl.ANY)
+    out, pg = pl.pallas_call(
+        layer_kernel,
+        out_shape=(
+            jax.ShapeDtypeStruct((mine, 4 * share * HD), jnp.bfloat16),
+            jax.ShapeDtypeStruct((4, 4) + policy_key.shape, policy_key.dtype),
+        ),
+        in_specs=[pl.BlockSpec(memory_space=pltpu.VMEM)] * 8,
+        out_specs=(any_space, any_space),
+        scratch_shapes=[
+            pltpu.VMEM((4, rows, depth), tokens.dtype),
+            pltpu.VMEM((4, 4 * block, width), ref_qkv.dtype),
+            pltpu.VMEM((rows, width), jnp.float32),
+            pltpu.VMEM((rows, HD), jnp.bfloat16),
+            pltpu.VMEM((rows, HD), jnp.bfloat16),
+            pltpu.VMEM((4, mine, share * HD), jnp.bfloat16),
+            pltpu.SemaphoreType.DMA((N_COPIES,)),
+            pltpu.SemaphoreType.DMA((N_COPIES,)),
+            pltpu.SemaphoreType.DMA((3,)),
+        ],
+        compiler_params=pltpu.CompilerParams(
+            collective_id=0, has_side_effects=True, vmem_limit_bytes=60 * 1024 * 1024
+        ),
+    )(tokens, ref_qkv, bias, cosine, sine, seg[:, None], seg[None, :], policy_key)
+    return out, pg.reshape((-1,) + policy_key.shape[1:])
+
+
+def per_group(tokens, ref_qkv, ref_bias, segment_ids, policy_key):
+    rank = lax.axis_index("rep")
+    width = ref_qkv.shape[1] // 4
+    bias = lax.dynamic_slice_in_dim(ref_bias, rank * width, width, 0)[None, :]
+    seg = segment_ids[0]
+    pos = positions_of(seg)
+    half = HD // 2
+    freq = 1000000.0 ** (-2.0 * jnp.arange(half, dtype=jnp.float32) / HD)
+    angle = pos.astype(jnp.float32)[:, None] * freq[None, :]
+    cosine, sine = jnp.cos(angle), jnp.sin(angle)
+    cosine = jnp.concatenate([cosine, cosine], axis=-1)
+    sine = jnp.concatenate([-sine, sine], axis=-1)
+    return whole_layer(tokens, ref_qkv, bias, cosine, sine, seg, policy_key)
+
+
 def solution(mesh):
     in_specs = (
         P("fsdp", "rep"),
@@ -91,6 +377,10 @@
         P(("rep", "fsdp"), "tp"),
     )
     out_specs = (P(("fsdp", "rep"), "tp"), P(None, "tp"))
+    shape = mesh.shape
+    grouped = (
+        shape["rep"] == 4 and shape["fsdp"] == 4 and shape["tp"] == 2 and KVH == shape["tp"] * shape["rep"]
+    )
     return jax.shard_map(
-        per_device, mesh=mesh, in_specs=in_specs, out_specs=out_specs, check_vma=False
-    )
+        per_group if grouped else per_device, mesh=mesh, in_specs=in_specs, out_specs=out_specs, check_vma=False
+    )

time: 531 us -> 220 us (0.41)
  waiting for transfers between devices: 443 us -> 0 us
  Pallas kernels: 0 us -> 203 us
  matrix products: 37.5 us -> 0 us
  local copies, waits for them, and re-layouts: 26.8 us -> 10.9 us
  between operations: 14.2 us -> 0.66 us
    reduce_scatter x1 -> x0, waiting for transfers between devices: 246 us -> none  [per_device(): lax.psum_scatter(partial_value, 'rep', scatter_dimension=0, tiled=True)]
    pallas_call x0 -> x1, Pallas kernels: none -> 203 us  [whole_layer(): pl.pallas_call(layer_kernel, out_shape=(jax.ShapeDtypeStruct((mine, 4 * s...]
    all_gather x5 -> x0, waiting for transfers between devices: 196 us -> none  [the longest x1 97.9 us: per_device(): lax.all_gather(ref_qkv, 'fsdp', axis=0, tiled=True)]
    dot_general x2 -> x0, matrix products: 25.4 us -> none  [the longest x1 15.2 us: per_device(): jnp.dot(tokens, lax.all_gather(ref_qkv, 'fsdp', axis=0, tiled=True), pref...]
    reshape x2 -> x0, local copies, waits for them, and re-layouts: 20.5 us -> none  [the longest x1 15.2 us: per_device(): partial_value = partial_value.reshape(rows, groups, share + 2, HD)]
    sub x1 -> x0, matrix products: 12.1 us -> none  [per_device(): expo = jnp.exp(scores - top)]
  transfers between devices with their start and end apart: 6 -> 0, of which waited for: 6 -> 0; matrix products, arithmetic and copies ran while one was open for 11% -> 0% of each run, Pallas kernels for 0% -> 0%
where the time goes in v2:
time: 220 us; the launch traced here: 219 us
  Pallas kernels  203 us (92%)
  local copies, waits for them, and re-layouts  10.9 us (5%)
  other arithmetic  4.53 us (2%)
    pallas_call x1, Pallas kernels, whole_layer(): pl.pallas_call(layer_kernel, out_shape=(jax.ShapeDtypeStruct((mine, 4 * s...  203 us
    unnamed x2, local copies, waits for them, and re-layouts  7.64 us

profile of v2, /device:TPU:0, one launch (start us, length us, event | category | flops | bytes accessed | tf_op | source)
XLA Modules:
  0.0 219.0 jit_solution(4716753038687867212)
XLA Ops:
  0.6 0.9 compare_reduce_fusion
  1.5 0.1 add_select_fusion
  1.6 0.3 reduce-window.9
  1.9 0.8 dynamic_slice.3
  2.6 0.6 broadcast_in_dim.9.bias
  3.2 0.1 slice.17
  3.3 0.1 slice_reduce_fusion
  3.5 0.1 fusion.1
  3.5 1.7 copy.7.seg_col
  5.2 1.9 fusion
  7.2 1.3 pad_maximum_fusion
  8.5 202.9 %shard_map.68 = (bf16[256,2560]{1,0:T(8,128)(2,1)}, bf16[4,4,320,512]{3,2,1,0:T(8,128)(2,1)}) custom-call(bf16[1024,1280]{1,0:T(8,128)(2,1)} %tok.1, bf16[320,3584]{1,0:T(8,128)(2,1)} %w.1, f32[1,896]{1,0:T(1,128)} %broadcast_in_dim.9.bias, f32[1024,128]{1,0:T(8,128)} %get-tuple-element.9.cosine, f32[1024,128]{1,0:T(8,128)} %get-tuple-element.10.sine, ...), custom_call_target="tpu_custom_call" | custom-call | tf_op jit(solution)/shard_map/pallas_call | solution.py:330
  211.3 2.5 %copy.10 = bf16[256,2560]{1,0:T(8,128)(2,1)} copy(bf16[256,2560]{1,0:T(8,128)(2,1)} %get-tuple-element.13) | data formatting | bytes 2621440
  213.8 5.2 %copy.11 = bf16[5120,512]{1,0:T(8,128)(2,1)} copy(bf16[5120,512]{1,0:T(8,128)(2,1)} %bitcast.10) | data formatting | bytes 10485760
  (2 shorter events, 0.0 us)

commit v3 on v2

--- a/solution.py
+++ b/solution.py
@@ -129,12 +129,12 @@
         pl.when(condition)(act)
 
 
-N_COPIES = 48
+N_COPIES = 57
 
 
 def layer_kernel(
     tok, w, bias, cosine, sine, seg_col, seg_row, pol, out, pg,
-    x, wg, proj, keys, vals, ctx, send, recv, local,
+    x, wg, proj, keys, vals, ctx, send, recv, local, ctx_send, ctx_recv,
 ):
     f, r, t, ahead, fx, fy = neighbours()
     to_x, to_y, partner = {"fsdp": fx}, {"fsdp": fy}, {"tp": 1 - t}
@@ -184,9 +184,10 @@
         pair[1].wait_recv()
         return [one, copies.start(b, b, to_x)]
 
-    part = pl.ds(pl.multiple_of(t * half, half), half)
-
-    def line(k):
+    parts = [pl.ds(pl.multiple_of(c * half + t * mine, mine), mine) for c in range(2)]
+
+    def line(k, c):
+        part = parts[c]
         below, above = source[k - 1], lax.rem(r + k - 1, 4)
         up_src = tok.at[part] if k == 1 else x.at[below, part]
         down_src = tok.at[part] if k == 1 else x.at[above, part]
@@ -198,29 +199,30 @@
         only(r >= k, pair[0].wait_recv)
         only(r <= 3 - k, pair[1].wait_recv)
 
-    def to_partner(k):
+    def to_partner(k, c):
+        part = parts[c]
         below, above = x.at[source[k], part], x.at[lax.rem(r + k, 4), part]
         return (
             copies.start(below, below, partner, r >= k),
             copies.start(above, above, partner, r <= 3 - k),
         )
 
-    def add(left, plane):
+    def add(left, plane, c):
         def tile(i, _):
-            at = pl.ds(pl.multiple_of(i * mine, mine), mine)
+            at = pl.ds(pl.multiple_of(c * half + i * mine, mine), mine)
             proj[at, :] += jnp.dot(left[at, :], wg[plane], preferred_element_type=jnp.float32)
             return 0
 
-        lax.fori_loop(0, 4, tile, 0)
-
-    def add_planes(k, pair):
+        lax.fori_loop(0, 2, tile, 0)
+
+    def add_planes(k, pair, c):
         def below():
             pair[0].wait_recv()
-            add(x.at[source[k]], source[k])
+            add(x.at[source[k]], source[k], c)
 
         def above():
             pair[1].wait_recv()
-            add(x.at[lax.rem(r + k, 4)], lax.rem(r + k, 4))
+            add(x.at[lax.rem(r + k, 4)], lax.rem(r + k, 4), c)
 
         only(r >= k, below)
         only(r <= 3 - k, above)
@@ -233,7 +235,7 @@
         for k in (1, 3, 2)
     }
     lo_z = policy_z(lo)
-    line1 = line(1)
+    near = line(1, 0)
     own_w.start()
     own_p.start()
     proj[...] = jnp.broadcast_to(bias[...], proj.shape)
@@ -247,26 +249,34 @@
     own_p.wait()
     lo_xy = policy_xy(lo, lo_z)
     weights_in += onward(3)
-    landed(1, line1)
-    line2 = line(2)
-    near = to_partner(1)
+    landed(1, near)
+    mid = line(2, 0)
+    near_late = line(1, 1)
+    shared_near = to_partner(1, 0)
     weights_in += onward(2)
     own_w.wait()
     for copy in weights_in[:2]:
         copy.wait_recv()
-    add(tok, r)
+    add(tok, r, 0)
+    landed(2, mid)
+    far = line(3, 0)
+    shared_mid = to_partner(2, 0)
+    landed(1, near_late)
+    mid_late = line(2, 1)
+    shared_near_late = to_partner(1, 1)
+    add(tok, r, 1)
     for copy in weights_in[2:]:
         copy.wait_recv()
-    landed(2, line2)
-    line3 = line(3)
-    mid = to_partner(2)
+    add_planes(1, shared_near, 0)
+    rest = policy_last(lo, lo_xy)
+    add_planes(2, shared_mid, 0)
+    landed(3, far)
+    shared_far = to_partner(3, 0)
+    landed(2, mid_late)
+    far_late = line(3, 1)
+    shared_mid_late = to_partner(2, 1)
     hi_z = policy_z(hi)
-    add_planes(1, near)
-    rest = policy_last(lo, lo_xy)
-    add_planes(2, mid)
-    landed(3, line3)
-    add_planes(3, to_partner(3))
-    hi_xy = policy_xy(hi, hi_z)
+    add_planes(3, shared_far, 0)
 
     def rotated(values, at):
         return values * cosine[at, :] + pltpu.roll(values, HD // 2, 1) * sine[at, :]
@@ -274,18 +284,26 @@
     def column(j):
         return pl.ds(pl.multiple_of(j * HD, HD), HD)
 
-    for i in range(4):
+    scale = 1.0 / math.sqrt(HD)
+
+    def rotate_keys(i):
         at = pl.ds(i * mine, mine)
         keys[at, :] = rotated(proj[at, column(share)], at).astype(jnp.bfloat16)
         vals[at, :] = proj[at, column(share + 1)].astype(jnp.bfloat16)
 
-    span = 3 * mine
-    scale = 1.0 / math.sqrt(HD)
-
-    def attend(k):
-        d = lax.rem(r + k, 4)
-        q0 = pl.multiple_of(d * mine, mine)
-        k0 = pl.multiple_of((d // 3) * mine, mine)
+    place = pl.ds(pl.multiple_of(r * share * HD, HD), share * HD)
+    own_c = pltpu.make_async_copy(ctx.at[r], out.at[:, place], local.at[2])
+
+    def send_context(d, step):
+        return pltpu.make_async_remote_copy(
+            src_ref=ctx.at[d], dst_ref=out.at[:, place],
+            send_sem=ctx_send.at[step], recv_sem=ctx_recv.at[step],
+            device_id={"rep": d}, device_id_type=MESH,
+        )
+
+    def attend(d):
+        first = max(d - 2, 0)
+        q0, k0, span = d * mine, first * mine, (d + 1 - first) * mine
         at, window = pl.ds(q0, mine), pl.ds(k0, span)
         q_index = q0 + lax.broadcasted_iota(jnp.int32, (mine, span), 0)
         k_index = k0 + lax.broadcasted_iota(jnp.int32, (mine, span), 1)
@@ -302,22 +320,35 @@
             expo = jnp.exp(scores - jnp.max(scores, axis=-1, keepdims=True))
             total = jnp.sum(expo, axis=-1, keepdims=True)
             weights = (expo * (1.0 / total)).astype(jnp.bfloat16)
-            ctx[k, :, c] = jnp.dot(weights, vv, preferred_element_type=jnp.float32).astype(jnp.bfloat16)
+            ctx[d, :, c] = jnp.dot(weights, vv, preferred_element_type=jnp.float32).astype(jnp.bfloat16)
             return 0
 
         lax.fori_loop(0, share, head, 0)
 
-    place = pl.ds(pl.multiple_of(r * share * HD, HD), share * HD)
-    for k in (2, 1, 3):
-        attend(k)
-        rest.append(copies.start(ctx.at[k], out.at[:, place], ahead[k]))
+        pl.when(r == d)(own_c.start)
+        pl.when(r != d)(send_context(d, lax.rem(d + 4 - r, 4)).start)
+
+    rotate_keys(0)
     attend(0)
-    own_c = pltpu.make_async_copy(ctx.at[0], out.at[:, place], local.at[2])
-    own_c.start()
+    rotate_keys(1)
+    attend(1)
+    add_planes(1, shared_near_late, 1)
+    add_planes(2, shared_mid_late, 1)
+    landed(3, far_late)
+    add_planes(3, to_partner(3, 1), 1)
+    rotate_keys(2)
+    rotate_keys(3)
+    attend(3)
+    attend(2)
+    hi_xy = policy_xy(hi, hi_z)
     rest += policy_last(hi, hi_xy)
     for copy in rest:
         copy.wait_recv()
     own_c.wait()
+    for k in (1, 2, 3):
+        copy = send_context(lax.rem(r + k, 4), k)
+        copy.wait_send()
+        copy.wait_recv()
     copies.finish()
 
 
@@ -345,6 +376,8 @@
             pltpu.SemaphoreType.DMA((N_COPIES,)),
             pltpu.SemaphoreType.DMA((N_COPIES,)),
             pltpu.SemaphoreType.DMA((3,)),
+            pltpu.SemaphoreType.DMA((4,)),
+            pltpu.SemaphoreType.DMA((4,)),
         ],
         compiler_params=pltpu.CompilerParams(
             collective_id=0, has_side_effects=True, vmem_limit_bytes=60 * 1024 * 1024

time: 220 us -> 233 us (1.059)
  Pallas kernels: 203 us -> 217 us
    pallas_call x1, Pallas kernels: 203 us -> 217 us  [whole_layer(): pl.pallas_call(layer_kernel, out_shape=(jax.ShapeDtypeStruct((mine, 4 * s...]
where the time goes in v3:
time: 233 us
  Pallas kernels  217 us (93%)
  local copies, waits for them, and re-layouts  10.9 us (5%)
  other arithmetic  4.53 us (2%)
    pallas_call x1, Pallas kernels, whole_layer(): pl.pallas_call(layer_kernel, out_shape=(jax.ShapeDtypeStruct((mine, 4 * s...  217 us
    unnamed x2, local copies, waits for them, and re-layouts  7.64 us

profile of v3, /device:TPU:0, one launch (start us, length us, event | category | flops | bytes accessed | tf_op | source)
XLA Modules:
  0.0 232.7 jit_solution(1347749315414169540)
XLA Ops:
  0.6 0.9 compare_reduce_fusion
  1.5 0.1 add_select_fusion
  1.6 0.3 reduce-window.9
  1.9 0.8 dynamic_slice.3
  2.6 0.6 broadcast_in_dim.9.bias
  3.2 0.1 slice.17
  3.3 0.1 slice_reduce_fusion
  3.5 0.1 fusion.1
  3.5 1.7 copy.7.seg_col
  5.2 1.9 fusion
  7.2 1.3 pad_maximum_fusion
  8.5 216.6 %shard_map.68 = (bf16[256,2560]{1,0:T(8,128)(2,1)}, bf16[4,4,320,512]{3,2,1,0:T(8,128)(2,1)}) custom-call(bf16[1024,1280]{1,0:T(8,128)(2,1)} %tok.1, bf16[320,3584]{1,0:T(8,128)(2,1)} %w.1, f32[1,896]{1,0:T(1,128)} %broadcast_in_dim.9.bias, f32[1024,128]{1,0:T(8,128)} %get-tuple-element.9.cosine, f32[1024,128]{1,0:T(8,128)} %get-tuple-element.10.sine, ...), custom_call_target="tpu_custom_call" | custom-call | tf_op jit(solution)/shard_map/pallas_call | solution.py:361
  225.1 2.5 %copy.10 = bf16[256,2560]{1,0:T(8,128)(2,1)} copy(bf16[256,2560]{1,0:T(8,128)(2,1)} %get-tuple-element.13) | data formatting | bytes 2621440
  227.5 5.2 %copy.11 = bf16[5120,512]{1,0:T(8,128)(2,1)} copy(bf16[5120,512]{1,0:T(8,128)(2,1)} %bitcast.10) | data formatting | bytes 10485760
  (2 shorter events, 0.0 us)

commit v4 on v3

--- a/solution.py
+++ b/solution.py
@@ -235,7 +235,9 @@
         for k in (1, 3, 2)
     }
     lo_z = policy_z(lo)
+    hi_z = policy_z(hi)
     near = line(1, 0)
+    near_late = line(1, 1)
     own_w.start()
     own_p.start()
     proj[...] = jnp.broadcast_to(bias[...], proj.shape)
@@ -246,37 +248,37 @@
     spread[2].wait_recv()
     passed[2] = across(held(2, f, 0, block), 2)
     weights_in += onward(1)
-    own_p.wait()
-    lo_xy = policy_xy(lo, lo_z)
     weights_in += onward(3)
     landed(1, near)
     mid = line(2, 0)
-    near_late = line(1, 1)
     shared_near = to_partner(1, 0)
     weights_in += onward(2)
+    own_p.wait()
+    lo_xy = policy_xy(lo, lo_z)
+    hi_xy = policy_xy(hi, hi_z)
     own_w.wait()
     for copy in weights_in[:2]:
         copy.wait_recv()
+    landed(1, near_late)
+    mid_late = line(2, 1)
+    shared_near_late = to_partner(1, 1)
     add(tok, r, 0)
+    add(tok, r, 1)
     landed(2, mid)
     far = line(3, 0)
     shared_mid = to_partner(2, 0)
-    landed(1, near_late)
-    mid_late = line(2, 1)
-    shared_near_late = to_partner(1, 1)
-    add(tok, r, 1)
     for copy in weights_in[2:]:
         copy.wait_recv()
     add_planes(1, shared_near, 0)
     rest = policy_last(lo, lo_xy)
     add_planes(2, shared_mid, 0)
-    landed(3, far)
-    shared_far = to_partner(3, 0)
     landed(2, mid_late)
     far_late = line(3, 1)
     shared_mid_late = to_partner(2, 1)
-    hi_z = policy_z(hi)
-    add_planes(3, shared_far, 0)
+    add_planes(1, shared_near_late, 1)
+    rest += policy_last(hi, hi_xy)
+    landed(3, far)
+    add_planes(3, to_partner(3, 0), 0)
 
     def rotated(values, at):
         return values * cosine[at, :] + pltpu.roll(values, HD // 2, 1) * sine[at, :]
@@ -332,7 +334,6 @@
     attend(0)
     rotate_keys(1)
     attend(1)
-    add_planes(1, shared_near_late, 1)
     add_planes(2, shared_mid_late, 1)
     landed(3, far_late)
     add_planes(3, to_partner(3, 1), 1)
@@ -340,8 +341,6 @@
     rotate_keys(3)
     attend(3)
     attend(2)
-    hi_xy = policy_xy(hi, hi_z)
-    rest += policy_last(hi, hi_xy)
     for copy in rest:
         copy.wait_recv()
     own_c.wait()

time: 233 us -> 211 us (0.906)
  Pallas kernels: 217 us -> 193 us
    pallas_call x1, Pallas kernels: 217 us -> 193 us  [whole_layer(): pl.pallas_call(layer_kernel, out_shape=(jax.ShapeDtypeStruct((mine, 4 * s...]
where the time goes in v4:
time: 211 us; the launch traced here: 209 us
  Pallas kernels  193 us (91%)
  local copies, waits for them, and re-layouts  10.9 us (5%)
  other arithmetic  4.53 us (2%)
    pallas_call x1, Pallas kernels, whole_layer(): pl.pallas_call(layer_kernel, out_shape=(jax.ShapeDtypeStruct((mine, 4 * s...  193 us
    unnamed x2, local copies, waits for them, and re-layouts  7.64 us

profile of v4, /device:TPU:0, one launch (start us, length us, event | category | flops | bytes accessed | tf_op | source)
XLA Modules:
  0.0 209.5 jit_solution(9785624281968355094)
XLA Ops:
  0.6 0.9 compare_reduce_fusion
  1.5 0.1 add_select_fusion
  1.6 0.3 reduce-window.9
  1.9 0.8 dynamic_slice.3
  2.6 0.6 broadcast_in_dim.9.bias
  3.2 0.1 slice.17
  3.3 0.1 slice_reduce_fusion
  3.5 0.1 fusion.1
  3.5 1.7 copy.7.seg_col
  5.2 1.9 fusion
  7.2 1.3 pad_maximum_fusion
  8.5 193.3 %shard_map.68 = (bf16[256,2560]{1,0:T(8,128)(2,1)}, bf16[4,4,320,512]{3,2,1,0:T(8,128)(2,1)}) custom-call(bf16[1024,1280]{1,0:T(8,128)(2,1)} %tok.1, bf16[320,3584]{1,0:T(8,128)(2,1)} %w.1, f32[1,896]{1,0:T(1,128)} %broadcast_in_dim.9.bias, f32[1024,128]{1,0:T(8,128)} %get-tuple-element.9.cosine, f32[1024,128]{1,0:T(8,128)} %get-tuple-element.10.sine, ...), custom_call_target="tpu_custom_call" | custom-call | tf_op jit(solution)/shard_map/pallas_call | solution.py:360
  201.8 2.5 %copy.10 = bf16[256,2560]{1,0:T(8,128)(2,1)} copy(bf16[256,2560]{1,0:T(8,128)(2,1)} %get-tuple-element.13) | data formatting | bytes 2621440
  204.3 5.2 %copy.11 = bf16[5120,512]{1,0:T(8,128)(2,1)} copy(bf16[5120,512]{1,0:T(8,128)(2,1)} %bitcast.10) | data formatting | bytes 10485760
  (2 shorter events, 0.0 us)
